TPU v7x, 256 devices: a whole 4x4x8 slice. The times are simulated.
256 devices in a mesh: dp: 16 (over x, z_lo, core), tensor: 16 (over z_hi, y).
Axes of the slice: x: 4, y: 4, z: 8 (z_hi: 4, z_lo: 2; z = z_hi * 2 + z_lo), core: 2. Of those that a mesh axis runs over, the one named last changes fastest.
Arguments:
- out_grad: bfloat16 [2, 1280, 4096], P(None, 'dp', 'tensor'), may hold values from -0.15625 to 0.15625
- layer_input: bfloat16 [2, 1280, 4096], P(None, 'dp', 'tensor'), may hold values from -8 to 8
- w_down: bfloat16 [16384, 4096], P('tensor'), may hold values from -0.046875 to 0.046875
- silu_gate: bfloat16 [2, 1280, 16384], P(None, 'dp', 'tensor'), may hold values from -6 to 6
- up_proj: bfloat16 [2, 1280, 16384], P(None, 'dp', 'tensor'), may hold values from -6 to 6
- slope_codes: int32 [2, 128, 16384], P(None, 'dp', 'tensor'), may hold values from 0 to 1073741823
Outputs:
- grad_down: bfloat16 [16384, 4096], P('tensor', 'dp')
- grad_gate: bfloat16 [4096, 16384], P('dp', 'tensor')
- grad_up: bfloat16 [4096, 16384], P('dp', 'tensor')
Inputs may be any that keep to these rules, and one draw needn't show every extreme that they name: `slope_codes`: every word holds ten independent 3-bit codes; all eight codes occur.
All inputs are finite; a program needn't handle non-finite values.
Results may differ from a plain program's by a relative error of at most 0.018.
Values may be sent and summed in bfloat16 or wider, within the bound.
A program may use at most 128 MiB of HBM per device.

v0:
```python
import jax
import jax.numpy as jnp
from jax import lax
from jax.sharding import PartitionSpec as P

SLOPE_LEVELS = (-0.09, 0.06, 0.22, 0.41, 0.6, 0.79, 0.96, 1.08)


def side_by_side(arrays, axis, dim, along):
    widths = [a.shape[along] for a in arrays]
    both = jnp.concatenate(arrays, axis=along)
    whole = lax.all_gather(both, axis, axis=dim, tiled=True)
    return tuple(jnp.split(whole, [sum(widths[:k]) for k in range(1, len(widths))], axis=along))


def decode_slopes(packed):
    shifts = 3 * jnp.arange(10, dtype=jnp.int32)
    pieces = jnp.bitwise_and(jnp.right_shift(packed[..., None, :], shifts[:, None]), 7)
    pieces = pieces.reshape(packed.shape[:-2] + (packed.shape[-2] * 10, packed.shape[-1]))
    result = jnp.full(pieces.shape, SLOPE_LEVELS[0], jnp.float32)
    for symbol in range(1, 8):
        result = jnp.where(pieces == symbol, jnp.float32(SLOPE_LEVELS[symbol]), result)
    return result


def shards(out_grad, layer_input, w_down, silu_gate, up_proj, slope_codes):
    micro_count = out_grad.shape[0]
    model_width = w_down.shape[1]
    hidden_width = w_down.shape[0]
    group_rows = micro_count * out_grad.shape[1]
    grad_rows, input_rows = side_by_side((out_grad, layer_input), "tensor", 2, 0)
    output_all = grad_rows.reshape(-1, model_width)
    input_all = input_rows.reshape(-1, model_width)
    gate_act = silu_gate.reshape(-1, hidden_width).astype(jnp.float32)
    up_value = up_proj.reshape(-1, hidden_width).astype(jnp.float32)
    hidden = (gate_act * up_value).astype(jnp.bfloat16)
    slopes = decode_slopes(slope_codes).reshape(-1, hidden_width)
    hidden_grad = lax.dot_general(
        output_all, w_down, (((1,), (1,)), ((), ())), preferred_element_type=jnp.float32
    )
    up_grad = (hidden_grad * gate_act).astype(jnp.bfloat16)
    gate_grad = (hidden_grad * up_value * slopes).astype(jnp.bfloat16)
    block_inputs, block_outputs = (
        lax.all_to_all(input_all, "dp", split_axis=1, concat_axis=0, tiled=True),
        lax.all_to_all(output_all, "dp", split_axis=1, concat_axis=0, tiled=True),
    )
    activations = jnp.concatenate((gate_grad, up_grad, hidden), axis=1)
    values = lax.all_gather(activations, "dp", axis=0, tiled=True)
    row_count = values.shape[0]
    groups = row_count // group_rows
    inputs_3d = block_inputs.reshape(groups, group_rows, block_inputs.shape[1])
    outputs_3d = block_outputs.reshape(groups, group_rows, block_outputs.shape[1])
    values_3d = values.reshape(groups, group_rows, values.shape[1])
    gate_up_parts = jnp.einsum(
        "grd,grf->gdf",
        inputs_3d,
        values_3d[:, :, : 2 * hidden_width],
        preferred_element_type=jnp.float32,
    )
    down_parts = jnp.einsum(
        "grf,grd->gfd",
        values_3d[:, :, 2 * hidden_width :],
        outputs_3d,
        preferred_element_type=jnp.float32,
    )
    gate_up_sum = jnp.sum(gate_up_parts.astype(jnp.bfloat16).astype(jnp.float32), axis=0)
    down_sum = jnp.sum(down_parts.astype(jnp.bfloat16).astype(jnp.float32), axis=0)
    grad_down = down_sum.astype(jnp.bfloat16)
    grad_gate = gate_up_sum[:, :hidden_width].astype(jnp.bfloat16)
    grad_up = gate_up_sum[:, hidden_width:].astype(jnp.bfloat16)
    return (grad_down, grad_gate, grad_up)


def solution(mesh):
    return jax.shard_map(
        shards,
        mesh=mesh,
        in_specs=(
            P(None, "dp", "tensor"),
            P(None, "dp", "tensor"),
            P("tensor", None),
            P(None, "dp", "tensor"),
            P(None, "dp", "tensor"),
            P(None, "dp", "tensor"),
        ),
        out_specs=(P("tensor", "dp"), P("dp", "tensor"), P("dp", "tensor")),
        check_vma=False,
    )
```

profile of v0, /device:TPU:1, one launch (start us, length us, event | category | flops | bytes accessed | tf_op | source)
XLA Modules:
  0.0 229.2 jit_solution(8711436910687394248)
XLA Ops:
  7.2 0.0 all-gather.3.cloned.1.call-start
  7.2 1.6 pad_maximum_fusion.1
  8.8 0.0 all-gather.3.cloned.1.call-update
  8.8 0.0 all-gather.5.cloned.1.call-start
  8.9 0.1 shift_right_arithmetic.28
  9.0 0.1 shift_right_arithmetic.30
  9.1 1.0 shift_right_arithmetic.25
  10.0 0.1 shift_right_arithmetic.26
  10.1 71.6 %all-gather.3.cloned.1.call-done = bf16[4,80,4096]{2,1,0:T(8,128)(2,1)} async-done(((bf16[4,80,256]{2,1,0:T(8,128)(2,1)}), bf16[4,80,4096]{2,1,0:T(8,128)(2,1)}) %all-gather.3.cloned.1.call-update) | async-done | bytes 2621456 | tf_op jit(solution)/shard_map/all_gather | solution.py:12
  81.7 0.0 copy-start
  81.7 0.0 copy-start.1
  81.7 1.9 fusion.8
  83.7 0.0 copy-done
  83.7 0.0 copy-done.1
  83.7 6.6 %fusion.6 = (bf16[160,1024]{1,0:T(8,128)(2,1)S(1)}, bf16[160,1024]{1,0:T(8,128)(2,1)S(1)}, bf16[160,1024]{1,0:T(8,128)(2,1)S(1)}) fusion(s32[160,1024]{1,0:T(8,128)S(1)} %shift_right_arithmetic.26, bf16[2,80,1024]{2,1,0:T(8,128)(2,1)S(1)} %copy-done, s32[160]{0:T(256)S(1)} %shift_right_arithmetic.30, bf16[2,80,1024]{2,1,0:T(8,128)(2,1)S(1)} %copy-done.1, ...), kind=kOutput, calls=%fused_computation.12 | convolution fusion | flops 1346273280 | bytes 11993728 | tf_op jit(solution)/shard_map/dot_general | solution.py:38
  90.3 1.0 pad_maximum_fusion
  91.3 0.0 all-gather.5.cloned.1.call-update
  91.3 0.3 copy.12
  91.7 1.5 copy.10
  93.2 5.7 %all-to-all-start.1 = ((bf16[160,16,256]{2,0,1:T(8,128)(2,1)}), bf16[160,16,256]{2,0,1:T(8,128)(2,1)S(1)}, u32[]{:S(2)}, u32[]{:S(2)}) async-start(bf16[160,16,256]{2,0,1:T(8,128)(2,1)} %copy.10), calls=%async_computation.1 | async-start | bytes 2621440 | tf_op jit(solution)/shard_map/all_to_all | solution.py:44
  98.9 0.3 copy.11
  99.2 1.5 copy.9
  100.7 28.8 %all-to-all-done.1 = bf16[160,16,256]{2,0,1:T(8,128)(2,1)S(1)} async-done(((bf16[160,16,256]{2,0,1:T(8,128)(2,1)}), bf16[160,16,256]{2,0,1:T(8,128)(2,1)S(1)}, u32[]{:S(2)}, u32[]{:S(2)}) %all-to-all-start.1) | async-done | bytes 1310752 | tf_op jit(solution)/shard_map/all_to_all | solution.py:44
  129.5 5.6 %all-to-all-start = ((bf16[160,16,256]{2,0,1:T(8,128)(2,1)}), bf16[160,16,256]{2,0,1:T(8,128)(2,1)S(1)}, u32[]{:S(2)}, u32[]{:S(2)}) async-start(bf16[160,16,256]{2,0,1:T(8,128)(2,1)} %copy.9), calls=%async_computation | async-start | bytes 2621440 | tf_op jit(solution)/shard_map/all_to_all | solution.py:45
  135.1 70.4 %all-gather.5.cloned.1.call-done = bf16[2560,3072]{1,0:T(8,128)(2,1)} async-done(((bf16[160,3072]{1,0:T(8,128)(2,1)}), bf16[2560,3072]{1,0:T(8,128)(2,1)}) %all-gather.5.cloned.1.call-update) | async-done | bytes 15728656 | tf_op jit(solution)/shard_map/all_gather | solution.py:48
  205.5 9.0 %convert_reduce_fusion = bf16[256,2048]{1,0:T(8,128)(2,1)S(1)} fusion(bf16[16,160,3072]{2,1,0:T(8,128)(2,1)} %bitcast.29, bf16[160,16,256]{2,0,1:T(8,128)(2,1)S(1)} %all-to-all-done.1), kind=kOutput, calls=%fused_computation | convolution fusion | flops 2700607488 | bytes 12845056 | tf_op jit(solution)/shard_map/grd,grf->gdf/dot_general | solution.py:54
  214.5 1.0 fusion.9
  215.6 0.0 all-to-all-done
  215.6 6.8 %convert_reduce_fusion.1 = bf16[1024,256]{1,0:T(8,128)(2,1)} fusion(bf16[16,160,3072]{2,1,0:T(8,128)(2,1)} %bitcast.30, bf16[160,16,256]{2,0,1:T(8,128)(2,1)S(1)} %all-to-all-done), kind=kOutput, calls=%fused_computation.2 | convolution fusion | flops 1350303744 | bytes 7077888 | tf_op jit(solution)/shard_map/grf,grd->gfd/dot_general | solution.py:60
  (3 shorter events, 0.0 us)
Async XLA Ops:
  7.2 74.5 %all-gather.3.cloned.1.call-start = ((), (), s32[]{:S(2)}) async-start(), calls=%async_computation.2 | async-start | bytes 2785280 | tf_op jit(solution)/shard_map/all_gather | solution.py:12
  8.8 196.7 %all-gather.5.cloned.1.call-start = ((), (), s32[]{:S(2)}) async-start(), calls=%async_computation.3 | async-start | bytes 16711680 | tf_op jit(solution)/shard_map/all_gather | solution.py:48
  81.7 2.0 copy-start
  81.7 2.0 copy-start.1
  93.2 36.3 %all-to-all-start.1 = ((bf16[160,16,256]{2,0,1:T(8,128)(2,1)}), bf16[160,16,256]{2,0,1:T(8,128)(2,1)S(1)}, u32[]{:S(2)}, u32[]{:S(2)}) async-start(bf16[160,16,256]{2,0,1:T(8,128)(2,1)} %copy.10), calls=%async_computation.1 | async-start | bytes 2621440 | tf_op jit(solution)/shard_map/all_to_all | solution.py:44
  129.5 86.0 %all-to-all-start = ((bf16[160,16,256]{2,0,1:T(8,128)(2,1)}), bf16[160,16,256]{2,0,1:T(8,128)(2,1)S(1)}, u32[]{:S(2)}, u32[]{:S(2)}) async-start(bf16[160,16,256]{2,0,1:T(8,128)(2,1)} %copy.9), calls=%async_computation | async-start | bytes 2621440 | tf_op jit(solution)/shard_map/all_to_all | solution.py:45
Sparse Core Ops, SparseCore 0:
  10.9 70.7 all-gather.2
  91.4 114.0 all-gather.4
where the time goes:
time: 230 us; the launch traced here: 229 us
  waiting for transfers between devices  171 us (74%)
  matrix products  22.4 us (10%)
  between operations  14.1 us (6%)
  starting transfers between devices  11.4 us (5%)
  local copies, waits for them, and re-layouts  7.94 us (3%)
  other arithmetic  2.63 us (1%)
    all_gather x1, waiting for transfers between devices, side_by_side(): whole = lax.all_gather(both, axis, axis=dim, tiled=True)  71.6 us
    all_gather x1, waiting for transfers between devices, shards(): values = lax.all_gather(activations, 'dp', axis=0, tiled=True)  70.4 us
    all_to_all x1, waiting for transfers between devices, shards(): lax.all_to_all(input_all, 'dp', split_axis=1, concat_axis=0, tiled=True)  28.8 us
    dot_general x1, matrix products, shards(): jnp.einsum('grd,grf->gdf', inputs_3d, values_3d[:, :, :2 * hidden_width],...  9 us
    dot_general x1, matrix products, shards(): jnp.einsum('grf,grd->gfd', values_3d[:, :, 2 * hidden_width:], outputs_3d...  6.77 us
    dot_general x1, matrix products, shards(): lax.dot_general(output_all, w_down, (((1,), (1,)), ((), ())), preferred_e...  6.59 us
    all_to_all x1, starting transfers between devices, shards(): lax.all_to_all(input_all, 'dp', split_axis=1, concat_axis=0, tiled=True)  5.68 us
    all_to_all x1, starting transfers between devices, shards(): lax.all_to_all(output_all, 'dp', split_axis=1, concat_axis=0, tiled=True)  5.61 us
  transfers between devices with their start and end apart: 4, of which 3 were waited for; matrix products, arithmetic and copies ran while one was open for 7% of the time, Pallas kernels for 0%

commit v1 on v0

v1 whole, which is shorter than its diff:
```python
import jax
import jax.numpy as jnp
from jax import lax
from jax.experimental import pallas as pl
from jax.experimental.pallas import tpu as pltpu
from jax.sharding import PartitionSpec as P

SLOPE_LEVELS = (-0.09, 0.06, 0.22, 0.41, 0.6, 0.79, 0.96, 1.08)
MESH = pl.DeviceIdType.MESH
ROWS = 160
HALF = 80
BLOCK = 256
HIDDEN = 1024
WIDTH = 4096
CHUNKS = 4
PART = HIDDEN // CHUNKS
WIDE = 2 * PART
N_COPIES = 128


def wrap(value):
    return lax.rem(value + 4, 4)


def kernel(
    dy_hbm, x_hbm, w_hbm, s_hbm, u_hbm, code_hbm,
    down_ref, gate_ref, up_ref,
    dyv, xv, wv, sv, uv, cv, rows, xt, dyt, hid, gu, h, slopes, xtt, dytt, psend, precv, pown,
    lsem, ssem, rsem, tsem,
):
    dp = lax.axis_index("dp")
    tensor = lax.axis_index("tensor")
    x, zl, c = dp // 4, lax.rem(dp // 2, 2), lax.rem(dp, 2)
    zh, y = tensor // 4, lax.rem(tensor, 4)
    y1, y0 = y // 2, lax.rem(y, 2)

    def device(x=x, zl=zl, c=c, zh=zh, y=y):
        return {"dp": x * 4 + zl * 2 + c, "tensor": zh * 4 + y}

    swap_x = device(zh, zl, y0, x, y1 * 2 + c)
    swap_d = {"dp": tensor, "tensor": dp}
    alone_x = jnp.logical_and(x == zh, c == y0)
    alone_d = dp == tensor
    ring = {
        "x+": device(x=wrap(x + 1)), "x-": device(x=wrap(x - 1)),
        "y+": device(y=wrap(y + 1)), "y-": device(y=wrap(y - 1)),
        "z+": device(zh=wrap(zh + 1)), "z-": device(zh=wrap(zh - 1)),
        "core": device(c=1 - c), "pair": device(zl=1 - zl),
    }

    barrier = pltpu.get_barrier_semaphore()
    for peer in ring.values():
        pl.semaphore_signal(barrier, inc=1, device_id=peer, device_id_type=MESH)

    @pl.when(jnp.logical_not(alone_x))
    def _():
        pl.semaphore_signal(barrier, inc=1, device_id=swap_x, device_id_type=MESH)

    @pl.when(jnp.logical_not(alone_d))
    def _():
        pl.semaphore_signal(barrier, inc=1, device_id=swap_d, device_id_type=MESH)

    local = [
        pltpu.make_async_copy(src, dst, lsem.at[i])
        for i, (src, dst) in enumerate(
            ((dy_hbm, dyv), (x_hbm, xv), (s_hbm, sv), (u_hbm, uv), (code_hbm, cv), (w_hbm, wv))
        )
    ]
    for copy in local:
        copy.start()

    sent = []

    def send(src, dst, peer):
        i = len(sent)
        copy = pltpu.make_async_remote_copy(
            src_ref=src, dst_ref=dst, send_sem=ssem.at[i], recv_sem=rsem.at[i], device_id=peer, device_id_type=MESH
        )
        copy.start()
        sent.append(copy)
        return copy

    def rows_at(buffer, row, start=0, size=ROWS):
        return buffer.at[pl.ds(pl.multiple_of(row * ROWS + start, 16), size)]

    def at_rows(zh, y, start=0, size=ROWS):
        return rows_at(rows, zh * 4 + y, start, size)

    def at_xt(zh, y, start=0, size=ROWS):
        return rows_at(xt, (y // 2) * 8 + zh * 2 + lax.rem(y, 2), start, size)

    def at_dyt(zh, y, start=0, size=ROWS):
        return rows_at(dyt, zh * 4 + y, start, size)

    class Gather:
        def __init__(self, at):
            self.at = at
            self.right, self.left, self.tops, self.bottoms = {}, {}, {}, {}
            self.origin = (zh, wrap(zh - 1), wrap(zh + 1), wrap(zh + 2))

        def along_y(self, b, first=None):
            block = self.at(self.origin[b], y)
            src = block if first is None else first
            self.right[b] = send(src, block, ring["y+"])
            self.left[b] = send(src, block, ring["y-"])

        def begin_z(self, first=None):
            block = self.at(zh, y)
            src = block if first is None else first
            self.zr = send(src, block, ring["z+"])
            self.zl = send(src, block, ring["z-"])

        def take_z_right(self):
            self.zr.wait_recv()
            half = self.at(self.origin[1], y, 0, HALF)
            self.zt = send(half, half, ring["z+"])

        def take_z_left(self):
            self.zl.wait_recv()
            half = self.at(self.origin[2], y, HALF, HALF)
            self.zb = send(half, half, ring["z-"])

        def take_z_far(self):
            self.zt.wait_recv()
            self.zb.wait_recv()

        def take_y(self, b):
            z = self.origin[b]
            self.right[b].wait_recv()
            half = self.at(z, wrap(y - 1), 0, HALF)
            self.tops[b] = send(half, half, ring["y+"])
            self.left[b].wait_recv()
            half = self.at(z, wrap(y + 1), HALF, HALF)
            self.bottoms[b] = send(half, half, ring["y-"])

        def take_y_far(self, b):
            self.tops[b].wait_recv()
            self.bottoms[b].wait_recv()

    class RingX:
        def __init__(self, at):
            self.at = at
            self.shared = []

        def begin(self):
            block = self.at(x, c)
            self.right = send(block, block, ring["x+"])
            self.left = send(block, block, ring["x-"])
            self.share(x)

        def share(self, origin):
            block = self.at(origin, c)
            self.shared.append(send(block, block, ring["core"]))

        def take(self):
            self.right.wait_recv()
            half = self.at(wrap(x - 1), c, 0, HALF)
            self.top = send(half, half, ring["x+"])
            self.left.wait_recv()
            half = self.at(wrap(x + 1), c, HALF, HALF)
            self.bottom = send(half, half, ring["x-"])
            self.share(wrap(x - 1))
            self.share(wrap(x + 1))

        def take_far(self):
            self.top.wait_recv()
            self.bottom.wait_recv()
            self.share(wrap(x + 2))

        def finish(self):
            for copy in self.shared:
                copy.wait_recv()

    local[2].wait()
    local[3].wait()
    own_hid = pl.ds(pl.multiple_of(dp * ROWS, 16), ROWS)
    hid[own_hid, :] = (sv[...].astype(jnp.float32) * uv[...].astype(jnp.float32)).astype(jnp.bfloat16)
    local[0].wait()
    local[1].wait()
    own_block = pltpu.make_async_copy(dyv, at_rows(zh, y), lsem.at[6])
    own_block.start()
    others = jnp.where(alone_x, 0, 1) + jnp.where(alone_d, 0, 1)
    pl.semaphore_wait(barrier, len(ring) + others)

    g_rows, g_x, g_d = Gather(at_rows), Gather(at_xt), Gather(at_dyt)
    g_rows.begin_z(dyv)
    g_rows.along_y(0, dyv)

    hid_own = RingX(lambda x, c, start=0, size=ROWS: rows_at(hid, x * 4 + zl * 2 + c, start, size))
    hid_pair = RingX(lambda x, c, start=0, size=ROWS: rows_at(hid, x * 4 + (1 - zl) * 2 + c, start, size))
    hid_own.begin()

    def transposed(src, dst, peer, alone, i):
        away = pltpu.make_async_remote_copy(
            src_ref=src, dst_ref=dst, send_sem=tsem.at[2 * i], recv_sem=tsem.at[2 * i + 1],
            device_id=peer, device_id_type=MESH,
        )
        here = pltpu.make_async_copy(src, dst, tsem.at[2 * i])

        @pl.when(jnp.logical_not(alone))
        def _():
            away.start()

        @pl.when(alone)
        def _():
            here.start()

        def wait():
            @pl.when(jnp.logical_not(alone))
            def _():
                away.wait()

            @pl.when(alone)
            def _():
                here.wait()

        return wait

    got_x = transposed(xv, at_xt(x, y1 * 2 + c), swap_x, alone_x, 0)
    got_d = transposed(dyv, rows_at(dyt, dp), swap_d, alone_d, 1)
    own = hid_own.at(x, c)
    pair = send(own, own, ring["pair"])

    local[4].wait()
    token = lax.broadcasted_iota(jnp.int32, (HALF, HALF), 0)
    place = lax.broadcasted_iota(jnp.int32, (HALF, HALF), 1)
    order = (place == lax.rem(token, 10) * 8 + token // 10).astype(jnp.float32).astype(jnp.bfloat16)
    for m in range(2):
        words = cv[m * 8 : m * 8 + 8, :]
        codes = jnp.concatenate(
            [jnp.bitwise_and(jnp.right_shift(words, 3 * k), 7).astype(jnp.float32) for k in range(10)], axis=0
        ).astype(jnp.bfloat16)
        codes = jnp.dot(order, codes, preferred_element_type=jnp.float32)
        level = jnp.full(codes.shape, SLOPE_LEVELS[0], jnp.float32)
        for symbol in range(1, 8):
            level = jnp.where(codes == jnp.float32(symbol), jnp.float32(SLOPE_LEVELS[symbol]), level)
        slopes[m * HALF : m * HALF + HALF, :] = level
    own_block.wait()
    local[5].wait()

    def multiply(z, y, first=False):
        block = at_rows(z, y)[...]
        weights = wv[:, pl.ds(pl.multiple_of((z * 4 + y) * BLOCK, BLOCK), BLOCK)]
        product = lax.dot_general(block, weights, (((1,), (1,)), ((), ())), preferred_element_type=jnp.float32)
        h[...] = product if first else h[...] + product

    multiply(zh, y, True)
    g_rows.take_z_right()
    g_rows.along_y(1)
    g_rows.take_z_left()
    g_rows.along_y(2)
    g_rows.take_y(0)
    g_rows.take_z_far()
    g_rows.along_y(3)
    got_x()
    g_x.begin_z()
    got_d()
    multiply(g_rows.origin[1], y)
    multiply(g_rows.origin[2], y)
    g_rows.take_y(1)
    multiply(g_rows.origin[3], y)
    multiply(zh, wrap(y - 1))
    multiply(zh, wrap(y + 1))
    hid_own.take()
    g_rows.take_y(2)
    multiply(g_rows.origin[1], wrap(y - 1))
    multiply(g_rows.origin[1], wrap(y + 1))
    pair.wait_recv()
    hid_pair.begin()
    g_x.take_z_right()
    g_x.take_z_left()
    g_x.take_z_far()
    g_d.begin_z()
    g_rows.take_y(3)
    for b in range(4):
        g_x.along_y(b)
    hid_own.take_far()
    g_rows.take_y_far(0)
    multiply(g_rows.origin[2], wrap(y - 1))
    multiply(g_rows.origin[2], wrap(y + 1))
    multiply(g_rows.origin[0], wrap(y + 2))
    g_rows.take_y_far(1)
    multiply(g_rows.origin[1], wrap(y + 2))
    multiply(g_rows.origin[3], wrap(y - 1))
    multiply(g_rows.origin[3], wrap(y + 1))
    g_rows.take_y_far(2)
    multiply(g_rows.origin[2], wrap(y + 2))
    g_rows.take_y_far(3)
    multiply(g_rows.origin[3], wrap(y + 2))

    def ring_of(k):
        return RingX(lambda x, c, start=0, size=ROWS: rows_at(gu.at[k], x * 2 + c, start, size))

    rings = [ring_of(k) for k in range(CHUNKS)]
    own_gu = pl.ds(pl.multiple_of((x * 2 + c) * ROWS, 16), ROWS)

    def activations(k):
        columns = slice(k * PART, (k + 1) * PART)
        grad = h[:, columns]
        gate = grad * uv[:, columns].astype(jnp.float32) * slopes[:, columns]
        gu[k, own_gu, 0:PART] = gate.astype(jnp.bfloat16)
        gu[k, own_gu, PART:WIDE] = (grad * sv[:, columns].astype(jnp.float32)).astype(jnp.bfloat16)

    for k in range(CHUNKS):
        activations(k)
        if k < 2:
            rings[k].begin()
    hid_pair.take()
    g_x.take_y(0)
    g_d.take_z_right()
    g_d.take_z_left()
    g_x.take_y(1)
    g_d.take_z_far()
    rings[0].take()
    g_x.take_y(2)
    rings[2].begin()
    g_x.take_y(3)
    hid_pair.take_far()
    for b in range(4):
        g_d.along_y(b)
    rings[1].take()
    rings[0].take_far()
    rings[3].begin()
    for b in range(4):
        g_x.take_y_far(b)
    for i in range(2):
        for r in range(5):
            xtt[i, :, r * 256 : (r + 1) * 256] = xt[i * 1280 + r * 256 : i * 1280 + (r + 1) * 256, :].T

    partials = []

    def products(k):
        rings[k].finish()
        values = gu[k]
        psend[k] = jnp.dot(xtt[1 - zl], values, preferred_element_type=jnp.float32).astype(jnp.bfloat16)
        partials.append(send(psend.at[k], precv.at[k], ring["pair"]))
        pown[k] = jnp.dot(xtt[zl], values, preferred_element_type=jnp.float32)

    def total(k):
        partials[k].wait_recv()
        whole = pown[k] + precv[k].astype(jnp.float32)
        columns = slice(k * PART, (k + 1) * PART)
        gate_ref[:, columns] = whole[:, 0:PART].astype(jnp.bfloat16)
        up_ref[:, columns] = whole[:, PART:WIDE].astype(jnp.bfloat16)

    products(0)
    rings[2].take()
    rings[1].take_far()
    g_d.take_y(0)
    products(1)
    rings[3].take()
    rings[2].take_far()
    g_d.take_y(1)
    g_d.take_y(2)
    products(2)
    g_d.take_y(3)
    rings[3].take_far()
    products(3)
    for b in range(4):
        g_d.take_y_far(b)
    hid_own.finish()
    hid_pair.finish()
    for r in range(10):
        dytt[:, r * 256 : (r + 1) * 256] = dyt[r * 256 : (r + 1) * 256, :].T
    for j in range(2):
        product = jnp.dot(dytt[...], hid[:, j * 512 : (j + 1) * 512], preferred_element_type=jnp.float32)
        down_ref[j * 512 : (j + 1) * 512, :] = product.T.astype(jnp.bfloat16)
    for k in range(CHUNKS):
        total(k)
    for copy in sent:
        copy.wait_send()


def shards(out_grad, layer_input, w_down, silu_gate, up_proj, slope_codes):
    bf16, f32 = jnp.bfloat16, jnp.float32
    vmem = pltpu.VMEM
    anywhere = pl.BlockSpec(memory_space=pl.ANY)
    down, gate, up = pl.pallas_call(
        kernel,
        out_shape=(
            jax.ShapeDtypeStruct((HIDDEN, BLOCK), bf16),
            jax.ShapeDtypeStruct((BLOCK, HIDDEN), bf16),
            jax.ShapeDtypeStruct((BLOCK, HIDDEN), bf16),
        ),
        in_specs=[anywhere] * 6,
        out_specs=[pl.BlockSpec(memory_space=pltpu.VMEM)] * 3,
        scratch_shapes=[
            vmem((ROWS, BLOCK), bf16),
            vmem((ROWS, BLOCK), bf16),
            vmem((HIDDEN, WIDTH), bf16),
            vmem((ROWS, HIDDEN), bf16),
            vmem((ROWS, HIDDEN), bf16),
            vmem((16, HIDDEN), jnp.int32),
            vmem((16 * ROWS, BLOCK), bf16),
            vmem((16 * ROWS, BLOCK), bf16),
            vmem((16 * ROWS, BLOCK), bf16),
            vmem((16 * ROWS, HIDDEN), bf16),
            vmem((CHUNKS, 8 * ROWS, WIDE), bf16),
            vmem((ROWS, HIDDEN), f32),
            vmem((ROWS, HIDDEN), f32),
            vmem((2, BLOCK, 8 * ROWS), bf16),
            vmem((BLOCK, 16 * ROWS), bf16),
            vmem((CHUNKS, BLOCK, WIDE), bf16),
            vmem((CHUNKS, BLOCK, WIDE), bf16),
            vmem((CHUNKS, BLOCK, WIDE), f32),
            pltpu.SemaphoreType.DMA((8,)),
            pltpu.SemaphoreType.DMA((N_COPIES,)),
            pltpu.SemaphoreType.DMA((N_COPIES,)),
            pltpu.SemaphoreType.DMA((4,)),
        ],
        compiler_params=pltpu.CompilerParams(
            collective_id=0, has_side_effects=True, vmem_limit_bytes=62 * 1024 * 1024
        ),
    )(
        out_grad.reshape(ROWS, BLOCK),
        layer_input.reshape(ROWS, BLOCK),
        w_down,
        silu_gate.reshape(ROWS, HIDDEN),
        up_proj.reshape(ROWS, HIDDEN),
        slope_codes.reshape(16, HIDDEN),
    )
    return down, gate, up


def solution(mesh):
    return jax.shard_map(
        shards,
        mesh=mesh,
        in_specs=(
            P(None, "dp", "tensor"),
            P(None, "dp", "tensor"),
            P("tensor", None),
            P(None, "dp", "tensor"),
            P(None, "dp", "tensor"),
            P(None, "dp", "tensor"),
        ),
        out_specs=(P("tensor", "dp"), P("dp", "tensor"), P("dp", "tensor")),
        check_vma=False,
    )
```

time: 230 us -> 102 us (0.44)
  the two profiles are of different devices: /device:TPU:1 before, /device:TPU:73 now
where the time goes in v1:
time: 102 us; the launch traced here: 101 us
  Pallas kernels  95.1 us (93%)
  local copies, waits for them, and re-layouts  5.6 us (5%)
    pallas_call x1, Pallas kernels, shards(): pl.pallas_call(kernel, out_shape=(jax.ShapeDtypeStruct((HIDDEN, BLOCK), b...  95.1 us
    unnamed x3, local copies, waits for them, and re-layouts  5.6 us

profile of v1, /device:TPU:73, one launch (start us, length us, event | category | flops | bytes accessed | tf_op | source)
XLA Modules:
  0.0 101.4 jit_solution(9560500905748146851)
XLA Ops:
  0.6 95.1 %shard_map.85 = (bf16[1024,256]{1,0:T(8,128)(2,1)}, bf16[256,1024]{1,0:T(8,128)(2,1)}, bf16[256,1024]{1,0:T(8,128)(2,1)}) custom-call(bf16[160,256]{1,0:T(8,128)(2,1)} %bitcast.7, bf16[160,256]{1,0:T(8,128)(2,1)} %bitcast.8, bf16[1024,4096]{1,0:T(8,128)(2,1)} %w_hbm.1, bf16[160,1024]{1,0:T(8,128)(2,1)} %bitcast.5, bf16[160,1024]{1,0:T(8,128)(2,1)} %bitcast.6, ...), custom_call_target="tpu_custom_call" | custom-call | tf_op jit(solution)/shard_map/pallas_call | solution.py:378
  95.8 1.9 %copy.12 = bf16[1024,256]{1,0:T(8,128)(2,1)} copy(bf16[1024,256]{1,0:T(8,128)(2,1)} %get-tuple-element.6) | data formatting | bytes 1048576
  97.6 1.9 %copy.13 = bf16[256,1024]{1,0:T(8,128)(2,1)} copy(bf16[256,1024]{1,0:T(8,128)(2,1)} %get-tuple-element.7) | data formatting | bytes 1048576
  99.5 1.9 %copy.14 = bf16[256,1024]{1,0:T(8,128)(2,1)} copy(bf16[256,1024]{1,0:T(8,128)(2,1)} %get-tuple-element.8) | data formatting | bytes 1048576

commit v2 on v0

v2 whole, which is shorter than its diff:
```python
import jax
import jax.numpy as jnp
from jax import lax
from jax.experimental import pallas as pl
from jax.experimental.pallas import tpu as pltpu
from jax.sharding import PartitionSpec as P

SLOPE_LEVELS = (-0.09, 0.06, 0.22, 0.41, 0.6, 0.79, 0.96, 1.08)
MESH = pl.DeviceIdType.MESH
ROWS = 160
HALF = 80
BLOCK = 256
HIDDEN = 1024
WIDTH = 4096
CHUNKS = 4
DOWN = 2
PIECES = DOWN + CHUNKS
PART = HIDDEN // CHUNKS
WIDE = 2 * PART
N_COPIES = 128


def wrap(value):
    return lax.rem(value + 4, 4)


def kernel(
    dy_hbm, x_hbm, w_hbm, s_hbm, u_hbm, code_hbm,
    down_hbm, gate_hbm, up_hbm,
    wv, sv, uv, cv, rows, xz, xt, dyt, relays, gu, h, slopes, xtt, dytt, psend, precv, pown,
    down_ref, gate_ref, up_ref, lsem, osem, ssem, rsem,
):
    dp = lax.axis_index("dp")
    tensor = lax.axis_index("tensor")
    x, zl, c = dp // 4, lax.rem(dp // 2, 2), lax.rem(dp, 2)
    zh, y = tensor // 4, lax.rem(tensor, 4)

    def device(x=x, zl=zl, c=c, zh=zh, y=y):
        return {"dp": x * 4 + zl * 2 + c, "tensor": zh * 4 + y}

    ring = {
        "x+": device(x=wrap(x + 1)), "x-": device(x=wrap(x - 1)),
        "y+": device(y=wrap(y + 1)), "y-": device(y=wrap(y - 1)),
        "z+": device(zh=wrap(zh + 1)), "z-": device(zh=wrap(zh - 1)),
        "core": device(c=1 - c), "pair": device(zl=1 - zl),
    }

    barrier = pltpu.get_barrier_semaphore()
    for peer in ring.values():
        pl.semaphore_signal(barrier, inc=1, device_id=peer, device_id_type=MESH)

    def rows_at(buffer, row, start=0, size=ROWS):
        return buffer.at[pl.ds(pl.multiple_of(row * ROWS + start, 16), size)]

    def at_rows(zh, y, start=0, size=ROWS):
        return rows_at(rows, zh * 4 + y, start, size)

    def at_xz(zh, y, start=0, size=ROWS):
        return rows_at(xz, zh, start, size)

    local = [
        pltpu.make_async_copy(src, dst, lsem.at[i])
        for i, (src, dst) in enumerate((
            (dy_hbm, at_rows(zh, y)), (x_hbm, at_xz(zh, y)), (s_hbm, sv), (u_hbm, uv), (code_hbm, cv), (w_hbm, wv)
        ))
    ]
    for copy in local:
        copy.start()

    sent = []

    def send(src, dst, peer):
        i = len(sent)
        copy = pltpu.make_async_remote_copy(
            src_ref=src, dst_ref=dst, send_sem=ssem.at[i], recv_sem=rsem.at[i],
            device_id=ring[peer], device_id_type=MESH,
        )
        copy.start()
        sent.append(copy)
        return copy

    class Ring:
        def __init__(self, at, me, axis):
            self.at, self.me, self.up, self.down = at, me, axis + "+", axis + "-"

        def begin(self, src=None):
            block = self.at(self.me)
            src = block if src is None else src
            self.right = send(src, block, self.up)
            self.left = send(src, block, self.down)

        def take(self):
            self.right.wait_recv()
            half = self.at(wrap(self.me - 1), 0, HALF)
            self.top = send(half, half, self.up)
            self.left.wait_recv()
            half = self.at(wrap(self.me + 1), HALF, HALF)
            self.bottom = send(half, half, self.down)

        def take_far(self):
            self.top.wait_recv()
            self.bottom.wait_recv()

    class Turn:
        def __init__(self, source, buffer, i):
            self.source, self.buffer, self.relay, self.i = source, buffer, relays.at[i], i
            self.origin = (x, wrap(x - 1), wrap(x + 1), wrap(x + 2))
            self.over_y = [
                Ring(lambda yo, start=0, size=ROWS, o=o: self.at(yo, o, start, size), y, "y") for o in self.origin
            ]

        def at(self, yo, xo, start=0, size=ROWS):
            return rows_at(self.buffer, yo * 8 + c * 4 + xo, start, size)

        def begin(self):
            self.kept = pltpu.make_async_copy(self.source(x), self.at(y, x), lsem.at[6 + self.i])
            self.kept.start()
            self.far_top = send(self.source(wrap(x + 2), 0, HALF), self.relay.at[0], "x+")
            self.far_bottom = send(self.source(wrap(x + 2), HALF, HALF), self.relay.at[1], "x-")
            self.right = send(self.source(wrap(x + 1)), self.at(y, x), "x+")
            self.left = send(self.source(wrap(x - 1)), self.at(y, x), "x-")

        def pass_on(self):
            self.far_top.wait_recv()
            self.top = send(self.relay.at[0], self.at(y, wrap(x - 1), 0, HALF), "x+")
            self.far_bottom.wait_recv()
            self.bottom = send(self.relay.at[1], self.at(y, wrap(x + 1), HALF, HALF), "x-")

        def along_y(self, b):
            if b == 0:
                self.kept.wait()
            elif b == 1:
                self.right.wait_recv()
            elif b == 2:
                self.left.wait_recv()
            else:
                self.top.wait_recv()
                self.bottom.wait_recv()
            self.over_y[b].begin()

        def share(self):
            self.shared = []
            for yo in (1 - c, 3 - c):
                block = self.buffer.at[pl.ds(pl.multiple_of((yo * 8 + c * 4) * ROWS, 16), 4 * ROWS)]
                self.shared.append(send(block, block, "core"))

        def finish(self):
            for copy in self.shared:
                copy.wait_recv()

        def turn(self, out):
            for i in range(2):
                for r in range(5):
                    start = pl.multiple_of((2 * i + c) * (8 * ROWS) + r * 256, 256)
                    out[i, :, r * 256 : (r + 1) * 256] = self.buffer[pl.ds(start, 256), :].T

    class Piece:
        def __init__(self, k):
            self.over_x = Ring(self.at(k), x, "x")
            self.shared = []

        def at(self, k):
            return lambda xo, start=0, size=ROWS: rows_at(gu.at[k], c * 4 + xo, start, size)

        def share(self, origin):
            block = self.over_x.at(origin)
            self.shared.append(send(block, block, "core"))

        def begin(self):
            self.over_x.begin()
            self.share(x)

        def take(self):
            self.over_x.take()
            self.share(wrap(x - 1))
            self.share(wrap(x + 1))

        def take_far(self):
            self.over_x.take_far()
            self.share(wrap(x + 2))

        def finish(self):
            for copy in self.shared:
                copy.wait_recv()

    own_rows = pl.ds(pl.multiple_of((c * 4 + x) * ROWS, 16), ROWS)
    local[2].wait()
    local[3].wait()
    for k in range(DOWN):
        columns = slice(k * WIDE, (k + 1) * WIDE)
        gu[k, own_rows, :] = (sv[:, columns].astype(jnp.float32) * uv[:, columns].astype(jnp.float32)).astype(jnp.bfloat16)
    local[0].wait()
    local[1].wait()
    pl.semaphore_wait(barrier, len(ring))

    origins = (zh, wrap(zh - 1), wrap(zh + 1), wrap(zh + 2))
    rows_z = Ring(lambda zo, start=0, size=ROWS: at_rows(zo, y, start, size), zh, "z")
    rows_y = [Ring(lambda yo, start=0, size=ROWS, o=o: at_rows(o, yo, start, size), y, "y") for o in origins]
    x_z = Ring(lambda zo, start=0, size=ROWS: at_xz(zo, y, start, size), zh, "z")
    turn_d = Turn(lambda zo, start=0, size=ROWS: at_rows(zo, y, start, size), dyt, 0)
    turn_x = Turn(lambda zo, start=0, size=ROWS: at_xz(zo, y, start, size), xt, 1)
    pieces = [Piece(k) for k in range(PIECES)]

    rows_z.begin()
    rows_y[0].begin()
    pieces[0].begin()
    pieces[1].begin()

    local[4].wait()
    token = lax.broadcasted_iota(jnp.int32, (HALF, HALF), 0)
    place = lax.broadcasted_iota(jnp.int32, (HALF, HALF), 1)
    order = (place == lax.rem(token, 10) * 8 + token // 10).astype(jnp.float32).astype(jnp.bfloat16)
    for m in range(2):
        words = cv[m * 8 : m * 8 + 8, :]
        codes = jnp.concatenate(
            [jnp.bitwise_and(jnp.right_shift(words, 3 * k), 7).astype(jnp.float32) for k in range(10)], axis=0
        ).astype(jnp.bfloat16)
        codes = jnp.dot(order, codes, preferred_element_type=jnp.float32)
        level = jnp.full(codes.shape, SLOPE_LEVELS[0], jnp.float32)
        for symbol in range(1, 8):
            level = jnp.where(codes == jnp.float32(symbol), jnp.float32(SLOPE_LEVELS[symbol]), level)
        slopes[m * HALF : m * HALF + HALF, :] = level
    local[5].wait()

    def multiply(b, yo, first=False):
        z = origins[b]
        weights = wv[:, pl.ds(pl.multiple_of((z * 4 + yo) * BLOCK, BLOCK), BLOCK)]
        product = lax.dot_general(
            at_rows(z, yo)[...], weights, (((1,), (1,)), ((), ())), preferred_element_type=jnp.float32
        )
        h[...] = product if first else h[...] + product

    def activations(k):
        columns = slice(k * PART, (k + 1) * PART)
        grad = h[:, columns]
        gate = grad * uv[:, columns].astype(jnp.float32) * slopes[:, columns]
        gu[DOWN + k, own_rows, 0:PART] = gate.astype(jnp.bfloat16)
        gu[DOWN + k, own_rows, PART:WIDE] = (grad * sv[:, columns].astype(jnp.float32)).astype(jnp.bfloat16)

    partials = {}
    outward = []

    def products(k):
        pieces[k].finish()
        lhs = dytt if k < DOWN else xtt
        values = gu[k]
        psend[k] = jnp.dot(lhs[1 - zl], values, preferred_element_type=jnp.float32).astype(jnp.bfloat16)
        partials[k] = send(psend.at[k], precv.at[k], "pair")
        pown[k] = jnp.dot(lhs[zl], values, preferred_element_type=jnp.float32)

    def put(src, dst):
        copy = pltpu.make_async_copy(src, dst, osem.at[len(outward)])
        copy.start()
        outward.append(copy)

    def total(k):
        partials[k].wait_recv()
        whole = pown[k] + precv[k].astype(jnp.float32)
        if k < DOWN:
            part = slice(k * WIDE, (k + 1) * WIDE)
            down_ref[part, :] = whole.T.astype(jnp.bfloat16)
            put(down_ref.at[part], down_hbm.at[part])
        else:
            part = slice((k - DOWN) * PART, (k - DOWN + 1) * PART)
            gate_ref[:, part] = whole[:, 0:PART].astype(jnp.bfloat16)
            put(gate_ref.at[:, part], gate_hbm.at[:, part])
            up_ref[:, part] = whole[:, PART:WIDE].astype(jnp.bfloat16)
            put(up_ref.at[:, part], up_hbm.at[:, part])

    multiply(0, y, True)
    rows_z.take()
    rows_y[1].begin()
    rows_y[2].begin()
    x_z.begin()
    rows_y[0].take()
    multiply(1, y)
    multiply(2, y)
    rows_z.take_far()
    rows_y[3].begin()
    turn_d.begin()
    pieces[0].take()
    multiply(3, y)
    multiply(0, wrap(y - 1))
    multiply(0, wrap(y + 1))
    rows_y[1].take()
    x_z.take()
    multiply(1, wrap(y - 1))
    multiply(1, wrap(y + 1))
    turn_d.pass_on()
    pieces[1].take()
    rows_y[2].take()
    multiply(2, wrap(y - 1))
    multiply(2, wrap(y + 1))
    x_z.take_far()
    turn_x.begin()
    rows_y[3].take()
    turn_d.along_y(0)
    turn_d.along_y(1)
    turn_d.along_y(2)
    turn_d.along_y(3)
    pieces[0].take_far()
    multiply(3, wrap(y - 1))
    multiply(3, wrap(y + 1))
    for b in range(4):
        rows_y[b].take_far()
        multiply(b, wrap(y + 2))
    for k in range(CHUNKS):
        activations(k)
        if k < 2:
            pieces[DOWN + k].begin()
    turn_x.pass_on()
    pieces[1].take_far()
    turn_d.over_y[0].take()
    turn_d.over_y[1].take()
    turn_x.along_y(0)
    turn_x.along_y(1)
    turn_d.over_y[2].take()
    turn_x.along_y(2)
    turn_d.over_y[3].take()
    turn_x.along_y(3)
    pieces[2].take()
    pieces[4].begin()
    for b in range(4):
        turn_d.over_y[b].take_far()
    turn_d.share()
    pieces[3].take()
    turn_x.over_y[0].take()
    turn_d.finish()
    turn_d.turn(dytt)
    products(0)
    pieces[2].take_far()
    pieces[5].begin()
    turn_x.over_y[1].take()
    products(1)
    turn_x.over_y[2].take()
    turn_x.over_y[3].take()
    pieces[4].take()
    pieces[3].take_far()
    for b in range(4):
        turn_x.over_y[b].take_far()
    turn_x.share()
    pieces[5].take()
    turn_x.finish()
    turn_x.turn(xtt)
    products(2)
    pieces[4].take_far()
    products(3)
    pieces[5].take_far()
    products(4)
    products(5)
    for k in range(PIECES):
        total(k)
    for copy in outward:
        copy.wait()
    for copy in sent:
        copy.wait_send()


def hand_over(*refs):
    for src, dst in zip(refs[:3], refs[3:]):
        dst[...] = src[...]


def shards(out_grad, layer_input, w_down, silu_gate, up_proj, slope_codes):
    bf16, f32 = jnp.bfloat16, jnp.float32
    vmem = pltpu.VMEM
    anywhere = pl.BlockSpec(memory_space=pl.ANY)
    results = pl.pallas_call(
        kernel,
        out_shape=(
            jax.ShapeDtypeStruct((HIDDEN, BLOCK), bf16),
            jax.ShapeDtypeStruct((BLOCK, HIDDEN), bf16),
            jax.ShapeDtypeStruct((BLOCK, HIDDEN), bf16),
        ),
        in_specs=[pl.BlockSpec(memory_space=pltpu.HBM)] * 6,
        out_specs=[anywhere] * 3,
        scratch_shapes=[
            vmem((HIDDEN, WIDTH), bf16),
            vmem((ROWS, HIDDEN), bf16),
            vmem((ROWS, HIDDEN), bf16),
            vmem((16, HIDDEN), jnp.int32),
            vmem((16 * ROWS, BLOCK), bf16),
            vmem((4 * ROWS, BLOCK), bf16),
            vmem((32 * ROWS, BLOCK), bf16),
            vmem((32 * ROWS, BLOCK), bf16),
            vmem((2, 2, HALF, BLOCK), bf16),
            vmem((PIECES, 8 * ROWS, WIDE), bf16),
            vmem((ROWS, HIDDEN), f32),
            vmem((ROWS, HIDDEN), f32),
            vmem((2, BLOCK, 8 * ROWS), bf16),
            vmem((2, BLOCK, 8 * ROWS), bf16),
            vmem((PIECES, BLOCK, WIDE), bf16),
            vmem((PIECES, BLOCK, WIDE), bf16),
            vmem((PIECES, BLOCK, WIDE), f32),
            vmem((HIDDEN, BLOCK), bf16),
            vmem((BLOCK, HIDDEN), bf16),
            vmem((BLOCK, HIDDEN), bf16),
            pltpu.SemaphoreType.DMA((8,)),
            pltpu.SemaphoreType.DMA((2 * CHUNKS + DOWN,)),
            pltpu.SemaphoreType.DMA((N_COPIES,)),
            pltpu.SemaphoreType.DMA((N_COPIES,)),
        ],
        compiler_params=pltpu.CompilerParams(
            collective_id=0, has_side_effects=True, vmem_limit_bytes=44 * 1024 * 1024
        ),
    )(
        out_grad.reshape(ROWS, BLOCK),
        layer_input.reshape(ROWS, BLOCK),
        w_down,
        silu_gate.reshape(ROWS, HIDDEN),
        up_proj.reshape(ROWS, HIDDEN),
        slope_codes.reshape(16, HIDDEN),
    )
    return pl.pallas_call(
        hand_over,
        out_shape=tuple(jax.ShapeDtypeStruct(a.shape, a.dtype) for a in results),
        in_specs=[pl.BlockSpec(memory_space=pltpu.VMEM)] * 3,
        out_specs=[pl.BlockSpec(memory_space=pltpu.VMEM)] * 3,
        compiler_params=pltpu.CompilerParams(vmem_limit_bytes=8 * 1024 * 1024),
    )(*results)


def solution(mesh):
    return jax.shard_map(
        shards,
        mesh=mesh,
        in_specs=(
            P(None, "dp", "tensor"),
            P(None, "dp", "tensor"),
            P("tensor", None),
            P(None, "dp", "tensor"),
            P(None, "dp", "tensor"),
            P(None, "dp", "tensor"),
        ),
        out_specs=(P("tensor", "dp"), P("dp", "tensor"), P("dp", "tensor")),
        check_vma=False,
    )
```

time: 230 us -> 91.6 us (0.40)
  waiting for transfers between devices: 171 us -> 0 us
  Pallas kernels: 0 us -> 86.1 us
  matrix products: 22.4 us -> 0 us
  between operations: 14.1 us -> 0.65 us
  starting transfers between devices: 11.4 us -> 0 us
  local copies, waits for them, and re-layouts: 7.94 us -> 4.55 us
  other arithmetic: 2.63 us -> 0 us
    all_gather x2 -> x0, waiting for transfers between devices: 142 us -> none  [the longest x1 71.6 us: side_by_side(): whole = lax.all_gather(both, axis, axis=dim, tiled=True)]
    pallas_call x0 -> x2, Pallas kernels: none -> 86.1 us  [the longest x1 84.9 us: shards(): pl.pallas_call(kernel, out_shape=(jax.ShapeDtypeStruct((HIDDEN, BLOCK), b...]
    all_to_all x2 -> x0, waiting for transfers between devices: 28.8 us -> none  [the longest x1 28.8 us: shards(): lax.all_to_all(input_all, 'dp', split_axis=1, concat_axis=0, tiled=True)]
    dot_general x3 -> x0, matrix products: 22.4 us -> none  [the longest x1 9 us: shards(): jnp.einsum('grd,grf->gdf', inputs_3d, values_3d[:, :, :2 * hidden_width],...]
    all_to_all x2 -> x0, starting transfers between devices: 11.3 us -> none  [the longest x1 5.68 us: shards(): lax.all_to_all(input_all, 'dp', split_axis=1, concat_axis=0, tiled=True)]
    unnamed x6 -> x10, local copies, waits for them, and re-layouts: 0.69 us -> 4.55 us
    all_to_all x2 -> x0, local copies, waits for them, and re-layouts: 3.04 us -> none  [the longest x1 1.52 us: shards(): lax.all_to_all(input_all, 'dp', split_axis=1, concat_axis=0, tiled=True)]
    concatenate x2 -> x0, other arithmetic: 2.62 us -> none  [the longest x1 1.61 us: side_by_side(): both = jnp.concatenate(arrays, axis=along)]
  transfers between devices with their start and end apart: 4 -> 0, of which waited for: 3 -> 0; matrix products, arithmetic and copies ran while one was open for 7% -> 0% of each run, Pallas kernels for 0% -> 0%
where the time goes in v2:
time: 91.6 us; the launch traced here: 91.3 us
  Pallas kernels  86.1 us (94%)
  local copies, waits for them, and re-layouts  4.55 us (5%)
    pallas_call x1, Pallas kernels, shards(): pl.pallas_call(kernel, out_shape=(jax.ShapeDtypeStruct((HIDDEN, BLOCK), b...  84.9 us
    unnamed x10, local copies, waits for them, and re-layouts  4.55 us

profile of v2, /device:TPU:1, one launch (start us, length us, event | category | flops | bytes accessed | tf_op | source)
XLA Modules:
  0.0 91.3 jit_solution(8684233705963707053)
XLA Ops:
  0.6 0.0 copy-start
  0.6 1.0 %copy-done = bf16[2,80,1024]{2,1,0:T(8,128)(2,1)S(1)} copy-done((bf16[2,80,1024]{2,1,0:T(8,128)(2,1)S(1)}, bf16[2,80,1024]{2,1,0:T(8,128)(2,1)}, u32[]{:S(2)}) %copy-start) | copy-done | bytes 327704
  1.6 0.0 copy-start.1
  1.6 1.0 %copy-done.1 = bf16[2,80,1024]{2,1,0:T(8,128)(2,1)S(1)} copy-done((bf16[2,80,1024]{2,1,0:T(8,128)(2,1)S(1)}, bf16[2,80,1024]{2,1,0:T(8,128)(2,1)}, u32[]{:S(2)}) %copy-start.1) | copy-done | bytes 327704
  2.6 0.0 copy-start.2
  2.6 0.9 copy-done.2
  3.5 0.0 copy-start.3
  3.5 0.9 copy-done.3
  4.4 0.0 copy-start.4
  4.4 0.8 copy-done.4
  5.2 84.9 %shard_map.85 = (bf16[1024,256]{1,0:T(8,128)(2,1)S(1)}, bf16[256,1024]{1,0:T(8,128)(2,1)S(1)}, bf16[256,1024]{1,0:T(8,128)(2,1)S(1)}) custom-call(bf16[160,256]{1,0:T(8,128)(2,1)S(1)} %bitcast.7, bf16[160,256]{1,0:T(8,128)(2,1)S(1)} %bitcast.8, bf16[1024,4096]{1,0:T(8,128)(2,1)} %w_hbm.1, bf16[160,1024]{1,0:T(8,128)(2,1)S(1)} %bitcast.5, ...), custom_call_target="tpu_custom_call" | custom-call | tf_op jit(solution)/shard_map/pallas_call | solution.py:368
  90.1 1.2 %shard_map.86 = (bf16[1024,256]{1,0:T(8,128)(2,1)}, bf16[256,1024]{1,0:T(8,128)(2,1)}, bf16[256,1024]{1,0:T(8,128)(2,1)}) custom-call(bf16[1024,256]{1,0:T(8,128)(2,1)S(1)} %get-tuple-element.6.refs_0_, bf16[256,1024]{1,0:T(8,128)(2,1)S(1)} %get-tuple-element.7.refs_1_, bf16[256,1024]{1,0:T(8,128)(2,1)S(1)} %get-tuple-element.8.refs_2_), custom_call_target="tpu_custom_call" | custom-call | tf_op jit(solution)/shard_map/pallas_call | solution.py:414
Async XLA Ops:
  0.6 1.0 %copy-start = (bf16[2,80,1024]{2,1,0:T(8,128)(2,1)S(1)}, bf16[2,80,1024]{2,1,0:T(8,128)(2,1)}, u32[]{:S(2)}) copy-start(bf16[2,80,1024]{2,1,0:T(8,128)(2,1)} %param.9) | copy-start | bytes 983044
  1.6 1.0 %copy-start.1 = (bf16[2,80,1024]{2,1,0:T(8,128)(2,1)S(1)}, bf16[2,80,1024]{2,1,0:T(8,128)(2,1)}, u32[]{:S(2)}) copy-start(bf16[2,80,1024]{2,1,0:T(8,128)(2,1)} %param.10) | copy-start | bytes 983044
  2.6 0.9 copy-start.2
  3.5 0.9 copy-start.3
  4.4 0.8 copy-start.4

commit v3 on v2

--- a/solution.py
+++ b/solution.py
@@ -17,7 +17,7 @@
 PIECES = DOWN + CHUNKS
 PART = HIDDEN // CHUNKS
 WIDE = 2 * PART
-N_COPIES = 128
+N_COPIES = 160
 
 
 def wrap(value):
@@ -80,14 +80,20 @@
         return copy
 
     class Ring:
-        def __init__(self, at, me, axis):
-            self.at, self.me, self.up, self.down = at, me, axis + "+", axis + "-"
-
-        def begin(self, src=None):
-            block = self.at(self.me)
-            src = block if src is None else src
-            self.right = send(src, block, self.up)
-            self.left = send(src, block, self.down)
+        def __init__(self, at, me, axis, split=False):
+            self.at, self.me, self.up, self.down, self.split = at, me, axis + "+", axis + "-", split
+
+        def begin(self):
+            if self.split:
+                top, bottom = self.at(self.me, 0, HALF), self.at(self.me, HALF, HALF)
+                self.right = send(top, top, self.up)
+                self.left = send(bottom, bottom, self.down)
+                self.rest = (send(bottom, bottom, self.up), send(top, top, self.down))
+            else:
+                block = self.at(self.me)
+                self.right = send(block, block, self.up)
+                self.left = send(block, block, self.down)
+                self.rest = ()
 
         def take(self):
             self.right.wait_recv()
@@ -96,6 +102,8 @@
             self.left.wait_recv()
             half = self.at(wrap(self.me + 1), HALF, HALF)
             self.bottom = send(half, half, self.down)
+            for copy in self.rest:
+                copy.wait_recv()
 
         def take_far(self):
             self.top.wait_recv()
@@ -105,6 +113,7 @@
         def __init__(self, source, buffer, i):
             self.source, self.buffer, self.relay, self.i = source, buffer, relays.at[i], i
             self.origin = (x, wrap(x - 1), wrap(x + 1), wrap(x + 2))
+            self.shared = []
             self.over_y = [
                 Ring(lambda yo, start=0, size=ROWS, o=o: self.at(yo, o, start, size), y, "y") for o in self.origin
             ]
@@ -138,10 +147,10 @@
                 self.bottom.wait_recv()
             self.over_y[b].begin()
 
-        def share(self):
-            self.shared = []
+        def arrive(self, b):
+            self.over_y[b].take_far()
             for yo in (1 - c, 3 - c):
-                block = self.buffer.at[pl.ds(pl.multiple_of((yo * 8 + c * 4) * ROWS, 16), 4 * ROWS)]
+                block = self.at(yo, self.origin[b])
                 self.shared.append(send(block, block, "core"))
 
         def finish(self):
@@ -194,9 +203,9 @@
     pl.semaphore_wait(barrier, len(ring))
 
     origins = (zh, wrap(zh - 1), wrap(zh + 1), wrap(zh + 2))
-    rows_z = Ring(lambda zo, start=0, size=ROWS: at_rows(zo, y, start, size), zh, "z")
+    rows_z = Ring(lambda zo, start=0, size=ROWS: at_rows(zo, y, start, size), zh, "z", True)
     rows_y = [Ring(lambda yo, start=0, size=ROWS, o=o: at_rows(o, yo, start, size), y, "y") for o in origins]
-    x_z = Ring(lambda zo, start=0, size=ROWS: at_xz(zo, y, start, size), zh, "z")
+    x_z = Ring(lambda zo, start=0, size=ROWS: at_xz(zo, y, start, size), zh, "z", True)
     turn_d = Turn(lambda zo, start=0, size=ROWS: at_rows(zo, y, start, size), dyt, 0)
     turn_x = Turn(lambda zo, start=0, size=ROWS: at_xz(zo, y, start, size), xt, 1)
     pieces = [Piece(k) for k in range(PIECES)]
@@ -276,79 +285,87 @@
     multiply(1, y)
     multiply(2, y)
     rows_z.take_far()
+    turn_d.begin()
     rows_y[3].begin()
-    turn_d.begin()
-    pieces[0].take()
     multiply(3, y)
     multiply(0, wrap(y - 1))
     multiply(0, wrap(y + 1))
     rows_y[1].take()
-    x_z.take()
+    turn_d.along_y(0)
     multiply(1, wrap(y - 1))
     multiply(1, wrap(y + 1))
+    rows_y[2].take()
     turn_d.pass_on()
-    pieces[1].take()
-    rows_y[2].take()
+    turn_d.along_y(1)
+    turn_d.along_y(2)
+    x_z.take()
+    rows_y[3].take()
     multiply(2, wrap(y - 1))
     multiply(2, wrap(y + 1))
+    turn_d.over_y[0].take()
+    turn_d.along_y(3)
+    pieces[0].take()
     x_z.take_far()
     turn_x.begin()
-    rows_y[3].take()
-    turn_d.along_y(0)
-    turn_d.along_y(1)
-    turn_d.along_y(2)
-    turn_d.along_y(3)
-    pieces[0].take_far()
     multiply(3, wrap(y - 1))
     multiply(3, wrap(y + 1))
-    for b in range(4):
+    for b in range(3):
         rows_y[b].take_far()
         multiply(b, wrap(y + 2))
-    for k in range(CHUNKS):
-        activations(k)
-        if k < 2:
-            pieces[DOWN + k].begin()
+    turn_d.over_y[1].take()
+    turn_d.over_y[2].take()
+    pieces[1].take()
     turn_x.pass_on()
-    pieces[1].take_far()
-    turn_d.over_y[0].take()
-    turn_d.over_y[1].take()
+    turn_d.arrive(0)
+    rows_y[3].take_far()
+    multiply(3, wrap(y + 2))
+    activations(0)
+    pieces[2].begin()
+    turn_d.over_y[3].take()
+    activations(1)
+    pieces[3].begin()
     turn_x.along_y(0)
     turn_x.along_y(1)
-    turn_d.over_y[2].take()
+    pieces[0].take_far()
     turn_x.along_y(2)
-    turn_d.over_y[3].take()
-    turn_x.along_y(3)
-    pieces[2].take()
-    pieces[4].begin()
-    for b in range(4):
-        turn_d.over_y[b].take_far()
-    turn_d.share()
-    pieces[3].take()
+    turn_d.arrive(1)
+    turn_d.arrive(2)
+    activations(2)
+    activations(3)
+    pieces[1].take_far()
+    turn_d.arrive(3)
     turn_x.over_y[0].take()
     turn_d.finish()
     turn_d.turn(dytt)
     products(0)
+    turn_x.along_y(3)
+    pieces[2].take()
+    products(1)
+    pieces[4].begin()
+    turn_x.over_y[1].take()
+    turn_x.over_y[2].take()
+    pieces[3].take()
+    turn_x.over_y[3].take()
+    turn_x.arrive(0)
     pieces[2].take_far()
     pieces[5].begin()
-    turn_x.over_y[1].take()
-    products(1)
-    turn_x.over_y[2].take()
-    turn_x.over_y[3].take()
+    turn_x.arrive(1)
+    turn_x.arrive(2)
     pieces[4].take()
-    pieces[3].take_far()
-    for b in range(4):
-        turn_x.over_y[b].take_far()
-    turn_x.share()
-    pieces[5].take()
+    turn_x.arrive(3)
     turn_x.finish()
     turn_x.turn(xtt)
     products(2)
+    pieces[3].take_far()
+    pieces[5].take()
+    products(3)
     pieces[4].take_far()
-    products(3)
+    products(4)
+    total(0)
+    total(1)
     pieces[5].take_far()
-    products(4)
     products(5)
-    for k in range(PIECES):
+    for k in range(DOWN, PIECES):
         total(k)
     for copy in outward:
         copy.wait()
@@ -404,12 +421,17 @@
             collective_id=0, has_side_effects=True, vmem_limit_bytes=44 * 1024 * 1024
         ),
     )(
-        out_grad.reshape(ROWS, BLOCK),
-        layer_input.reshape(ROWS, BLOCK),
-        w_down,
-        silu_gate.reshape(ROWS, HIDDEN),
-        up_proj.reshape(ROWS, HIDDEN),
-        slope_codes.reshape(16, HIDDEN),
+        *(
+            pltpu.with_memory_space_constraint(a, pltpu.HBM)
+            for a in (
+                out_grad.reshape(ROWS, BLOCK),
+                layer_input.reshape(ROWS, BLOCK),
+                w_down,
+                silu_gate.reshape(ROWS, HIDDEN),
+                up_proj.reshape(ROWS, HIDDEN),
+                slope_codes.reshape(16, HIDDEN),
+            )
+        )
     )
     return pl.pallas_call(
         hand_over,

time: 91.6 us -> 82.1 us (0.90)
  Pallas kernels: 86.1 us -> 81.4 us
  local copies, waits for them, and re-layouts: 4.55 us -> 0 us
    pallas_call x1, Pallas kernels: 84.9 us -> 80.2 us  [shards(): pl.pallas_call(kernel, out_shape=(jax.ShapeDtypeStruct((HIDDEN, BLOCK), b...]
    unnamed x10 -> x0, local copies, waits for them, and re-layouts: 4.55 us -> none
where the time goes in v3:
time: 82.1 us
  Pallas kernels  81.4 us (99%)
    pallas_call x1, Pallas kernels, shards(): pl.pallas_call(kernel, out_shape=(jax.ShapeDtypeStruct((HIDDEN, BLOCK), b...  80.2 us

profile of v3, /device:TPU:1, one launch (start us, length us, event | category | flops | bytes accessed | tf_op | source)
XLA Modules:
  0.0 82.1 jit_solution(16627896815009732650)
XLA Ops:
  0.6 80.2 %shard_map.85 = (bf16[1024,256]{1,0:T(8,128)(2,1)S(1)}, bf16[256,1024]{1,0:T(8,128)(2,1)S(1)}, bf16[256,1024]{1,0:T(8,128)(2,1)S(1)}) custom-call(bf16[160,256]{1,0:T(8,128)(2,1)} %bitcast.7, bf16[160,256]{1,0:T(8,128)(2,1)} %bitcast.8, bf16[1024,4096]{1,0:T(8,128)(2,1)} %w_hbm.1, bf16[160,1024]{1,0:T(8,128)(2,1)} %bitcast.5, bf16[160,1024]{1,0:T(8,128)(2,1)} %bitcast.6, ...), custom_call_target="tpu_custom_call" | custom-call | tf_op jit(solution)/shard_map/pallas_call | solution.py:385
  80.8 1.2 %shard_map.86 = (bf16[1024,256]{1,0:T(8,128)(2,1)}, bf16[256,1024]{1,0:T(8,128)(2,1)}, bf16[256,1024]{1,0:T(8,128)(2,1)}) custom-call(bf16[1024,256]{1,0:T(8,128)(2,1)S(1)} %get-tuple-element.6.refs_0_, bf16[256,1024]{1,0:T(8,128)(2,1)S(1)} %get-tuple-element.7.refs_1_, bf16[256,1024]{1,0:T(8,128)(2,1)S(1)} %get-tuple-element.8.refs_2_), custom_call_target="tpu_custom_call" | custom-call | tf_op jit(solution)/shard_map/pallas_call | solution.py:436

commit v4 on v3

--- a/solution.py
+++ b/solution.py
@@ -17,7 +17,8 @@
 PIECES = DOWN + CHUNKS
 PART = HIDDEN // CHUNKS
 WIDE = 2 * PART
-N_COPIES = 160
+N_SENDS = 48
+N_SLOTS = 88
 
 
 def wrap(value):
@@ -69,19 +70,34 @@
 
     sent = []
 
-    def send(src, dst, peer):
+    slots = []
+
+    def slot():
+        slots.append(len(slots))
+        return slots[-1]
+
+    def send(src, dst, peer, into=None):
         i = len(sent)
+        if i >= N_SENDS:
+            sent[i - N_SENDS].wait_send()
         copy = pltpu.make_async_remote_copy(
-            src_ref=src, dst_ref=dst, send_sem=ssem.at[i], recv_sem=rsem.at[i],
+            src_ref=src, dst_ref=dst, send_sem=ssem.at[i % N_SENDS], recv_sem=rsem.at[slot() if into is None else into],
             device_id=ring[peer], device_id_type=MESH,
         )
         copy.start()
         sent.append(copy)
         return copy
 
+    def landed(block, into):
+        pltpu.make_async_remote_copy(
+            src_ref=block, dst_ref=block, send_sem=ssem.at[0], recv_sem=rsem.at[into],
+            device_id=ring["core"], device_id_type=MESH,
+        ).wait_recv()
+
     class Ring:
         def __init__(self, at, me, axis, split=False):
             self.at, self.me, self.up, self.down, self.split = at, me, axis + "+", axis + "-", split
+            self.far = slot()
 
         def begin(self):
             if self.split:
@@ -98,22 +114,21 @@
         def take(self):
             self.right.wait_recv()
             half = self.at(wrap(self.me - 1), 0, HALF)
-            self.top = send(half, half, self.up)
+            send(half, half, self.up, self.far)
             self.left.wait_recv()
             half = self.at(wrap(self.me + 1), HALF, HALF)
-            self.bottom = send(half, half, self.down)
+            send(half, half, self.down, self.far)
             for copy in self.rest:
                 copy.wait_recv()
 
         def take_far(self):
-            self.top.wait_recv()
-            self.bottom.wait_recv()
+            landed(self.at(wrap(self.me + 2)), self.far)
 
     class Turn:
         def __init__(self, source, buffer, i):
             self.source, self.buffer, self.relay, self.i = source, buffer, relays.at[i], i
             self.origin = (x, wrap(x - 1), wrap(x + 1), wrap(x + 2))
-            self.shared = []
+            self.far, self.core = slot(), slot()
             self.over_y = [
                 Ring(lambda yo, start=0, size=ROWS, o=o: self.at(yo, o, start, size), y, "y") for o in self.origin
             ]
@@ -131,9 +146,9 @@
 
         def pass_on(self):
             self.far_top.wait_recv()
-            self.top = send(self.relay.at[0], self.at(y, wrap(x - 1), 0, HALF), "x+")
+            send(self.relay.at[0], self.at(y, wrap(x - 1), 0, HALF), "x+", self.far)
             self.far_bottom.wait_recv()
-            self.bottom = send(self.relay.at[1], self.at(y, wrap(x + 1), HALF, HALF), "x-")
+            send(self.relay.at[1], self.at(y, wrap(x + 1), HALF, HALF), "x-", self.far)
 
         def along_y(self, b):
             if b == 0:
@@ -143,19 +158,17 @@
             elif b == 2:
                 self.left.wait_recv()
             else:
-                self.top.wait_recv()
-                self.bottom.wait_recv()
+                landed(self.at(y, wrap(x + 2)), self.far)
             self.over_y[b].begin()
 
         def arrive(self, b):
             self.over_y[b].take_far()
             for yo in (1 - c, 3 - c):
                 block = self.at(yo, self.origin[b])
-                self.shared.append(send(block, block, "core"))
+                send(block, block, "core", self.core)
 
         def finish(self):
-            for copy in self.shared:
-                copy.wait_recv()
+            landed(self.buffer.at[pl.ds(pl.multiple_of(c * (8 * ROWS), 16), 8 * ROWS)], self.core)
 
         def turn(self, out):
             for i in range(2):
@@ -165,15 +178,16 @@
 
     class Piece:
         def __init__(self, k):
+            self.k = k
             self.over_x = Ring(self.at(k), x, "x")
-            self.shared = []
+            self.core = slot()
 
         def at(self, k):
             return lambda xo, start=0, size=ROWS: rows_at(gu.at[k], c * 4 + xo, start, size)
 
         def share(self, origin):
             block = self.over_x.at(origin)
-            self.shared.append(send(block, block, "core"))
+            send(block, block, "core", self.core)
 
         def begin(self):
             self.over_x.begin()
@@ -189,8 +203,7 @@
             self.share(wrap(x + 2))
 
         def finish(self):
-            for copy in self.shared:
-                copy.wait_recv()
+            landed(gu.at[self.k].at[pl.ds(pl.multiple_of((1 - c) * (4 * ROWS), 16), 4 * ROWS)], self.core)
 
     own_rows = pl.ds(pl.multiple_of((c * 4 + x) * ROWS, 16), ROWS)
     local[2].wait()
@@ -287,11 +300,11 @@
     rows_z.take_far()
     turn_d.begin()
     rows_y[3].begin()
+    turn_d.along_y(0)
     multiply(3, y)
     multiply(0, wrap(y - 1))
     multiply(0, wrap(y + 1))
     rows_y[1].take()
-    turn_d.along_y(0)
     multiply(1, wrap(y - 1))
     multiply(1, wrap(y + 1))
     rows_y[2].take()
@@ -302,8 +315,8 @@
     rows_y[3].take()
     multiply(2, wrap(y - 1))
     multiply(2, wrap(y + 1))
+    turn_d.along_y(3)
     turn_d.over_y[0].take()
-    turn_d.along_y(3)
     pieces[0].take()
     x_z.take_far()
     turn_x.begin()
@@ -315,10 +328,10 @@
     turn_d.over_y[1].take()
     turn_d.over_y[2].take()
     pieces[1].take()
-    turn_x.pass_on()
     turn_d.arrive(0)
     rows_y[3].take_far()
     multiply(3, wrap(y + 2))
+    turn_x.pass_on()
     activations(0)
     pieces[2].begin()
     turn_d.over_y[3].take()
@@ -334,10 +347,10 @@
     activations(3)
     pieces[1].take_far()
     turn_d.arrive(3)
-    turn_x.over_y[0].take()
     turn_d.finish()
     turn_d.turn(dytt)
     products(0)
+    turn_x.over_y[0].take()
     turn_x.along_y(3)
     pieces[2].take()
     products(1)
@@ -367,9 +380,10 @@
     products(5)
     for k in range(DOWN, PIECES):
         total(k)
+    assert len(slots) <= N_SLOTS
     for copy in outward:
         copy.wait()
-    for copy in sent:
+    for copy in sent[-N_SENDS:]:
         copy.wait_send()
 
 
@@ -414,8 +428,8 @@
             vmem((BLOCK, HIDDEN), bf16),
             pltpu.SemaphoreType.DMA((8,)),
             pltpu.SemaphoreType.DMA((2 * CHUNKS + DOWN,)),
-            pltpu.SemaphoreType.DMA((N_COPIES,)),
-            pltpu.SemaphoreType.DMA((N_COPIES,)),
+            pltpu.SemaphoreType.DMA((N_SENDS,)),
+            pltpu.SemaphoreType.DMA((N_SLOTS,)),
         ],
         compiler_params=pltpu.CompilerParams(
             collective_id=0, has_side_effects=True, vmem_limit_bytes=44 * 1024 * 1024

time: 82.1 us -> 80.1 us (0.976)
  Pallas kernels: 81.4 us -> 79.4 us
    pallas_call x1, Pallas kernels: 80.2 us -> 78.1 us  [shards(): pl.pallas_call(kernel, out_shape=(jax.ShapeDtypeStruct((HIDDEN, BLOCK), b...]
where the time goes in v4:
time: 80.1 us; the launch traced here: 80 us
  Pallas kernels  79.4 us (99%)
    pallas_call x1, Pallas kernels, shards(): pl.pallas_call(kernel, out_shape=(jax.ShapeDtypeStruct((HIDDEN, BLOCK), b...  78.1 us

profile of v4, /device:TPU:1, one launch (start us, length us, event | category | flops | bytes accessed | tf_op | source)
XLA Modules:
  0.0 80.0 jit_solution(14032903631063026838)
XLA Ops:
  0.6 78.1 %shard_map.85 = (bf16[1024,256]{1,0:T(8,128)(2,1)S(1)}, bf16[256,1024]{1,0:T(8,128)(2,1)S(1)}, bf16[256,1024]{1,0:T(8,128)(2,1)S(1)}) custom-call(bf16[160,256]{1,0:T(8,128)(2,1)} %bitcast.7, bf16[160,256]{1,0:T(8,128)(2,1)} %bitcast.8, bf16[1024,4096]{1,0:T(8,128)(2,1)} %w_hbm.1, bf16[160,1024]{1,0:T(8,128)(2,1)} %bitcast.5, bf16[160,1024]{1,0:T(8,128)(2,1)} %bitcast.6, ...), custom_call_target="tpu_custom_call" | custom-call | tf_op jit(solution)/shard_map/pallas_call | solution.py:399
  78.8 1.2 %shard_map.86 = (bf16[1024,256]{1,0:T(8,128)(2,1)}, bf16[256,1024]{1,0:T(8,128)(2,1)}, bf16[256,1024]{1,0:T(8,128)(2,1)}) custom-call(bf16[1024,256]{1,0:T(8,128)(2,1)S(1)} %get-tuple-element.6.refs_0_, bf16[256,1024]{1,0:T(8,128)(2,1)S(1)} %get-tuple-element.7.refs_1_, bf16[256,1024]{1,0:T(8,128)(2,1)S(1)} %get-tuple-element.8.refs_2_), custom_call_target="tpu_custom_call" | custom-call | tf_op jit(solution)/shard_map/pallas_call | solution.py:450

commit v5 on v4

--- a/solution.py
+++ b/solution.py
@@ -305,36 +305,36 @@
     multiply(0, wrap(y - 1))
     multiply(0, wrap(y + 1))
     rows_y[1].take()
-    multiply(1, wrap(y - 1))
-    multiply(1, wrap(y + 1))
+    turn_d.pass_on()
     rows_y[2].take()
-    turn_d.pass_on()
     turn_d.along_y(1)
     turn_d.along_y(2)
     x_z.take()
+    turn_d.along_y(3)
     rows_y[3].take()
+    turn_d.over_y[0].take()
+    multiply(1, wrap(y - 1))
+    multiply(1, wrap(y + 1))
     multiply(2, wrap(y - 1))
     multiply(2, wrap(y + 1))
-    turn_d.along_y(3)
-    turn_d.over_y[0].take()
     pieces[0].take()
+    pieces[1].take()
     x_z.take_far()
     turn_x.begin()
+    turn_d.over_y[1].take()
+    turn_d.over_y[2].take()
     multiply(3, wrap(y - 1))
     multiply(3, wrap(y + 1))
     for b in range(3):
         rows_y[b].take_far()
         multiply(b, wrap(y + 2))
-    turn_d.over_y[1].take()
-    turn_d.over_y[2].take()
-    pieces[1].take()
-    turn_d.arrive(0)
+    turn_d.over_y[3].take()
+    turn_x.pass_on()
     rows_y[3].take_far()
     multiply(3, wrap(y + 2))
-    turn_x.pass_on()
     activations(0)
     pieces[2].begin()
-    turn_d.over_y[3].take()
+    turn_d.arrive(0)
     activations(1)
     pieces[3].begin()
     turn_x.along_y(0)
@@ -343,13 +343,13 @@
     turn_x.along_y(2)
     turn_d.arrive(1)
     turn_d.arrive(2)
-    activations(2)
-    activations(3)
-    pieces[1].take_far()
     turn_d.arrive(3)
     turn_d.finish()
     turn_d.turn(dytt)
     products(0)
+    pieces[1].take_far()
+    activations(2)
+    activations(3)
     turn_x.over_y[0].take()
     turn_x.along_y(3)
     pieces[2].take()

time: 80.1 us -> 79.3 us (0.990)
  no operation moved by 1% of the time
where the time goes in v5:
time: 79.3 us; the launch traced here: 79.2 us
  Pallas kernels  78.6 us (99%)
    pallas_call x1, Pallas kernels, shards(): pl.pallas_call(kernel, out_shape=(jax.ShapeDtypeStruct((HIDDEN, BLOCK), b...  77.4 us

profile of v5, /device:TPU:1, one launch (start us, length us, event | category | flops | bytes accessed | tf_op | source)
XLA Modules:
  0.0 79.2 jit_solution(9913213827040657350)
XLA Ops:
  0.6 77.4 %shard_map.85 = (bf16[1024,256]{1,0:T(8,128)(2,1)S(1)}, bf16[256,1024]{1,0:T(8,128)(2,1)S(1)}, bf16[256,1024]{1,0:T(8,128)(2,1)S(1)}) custom-call(bf16[160,256]{1,0:T(8,128)(2,1)} %bitcast.7, bf16[160,256]{1,0:T(8,128)(2,1)} %bitcast.8, bf16[1024,4096]{1,0:T(8,128)(2,1)} %w_hbm.1, bf16[160,1024]{1,0:T(8,128)(2,1)} %bitcast.5, bf16[160,1024]{1,0:T(8,128)(2,1)} %bitcast.6, ...), custom_call_target="tpu_custom_call" | custom-call | tf_op jit(solution)/shard_map/pallas_call | solution.py:399
  78.0 1.2 %shard_map.86 = (bf16[1024,256]{1,0:T(8,128)(2,1)}, bf16[256,1024]{1,0:T(8,128)(2,1)}, bf16[256,1024]{1,0:T(8,128)(2,1)}) custom-call(bf16[1024,256]{1,0:T(8,128)(2,1)S(1)} %get-tuple-element.6.refs_0_, bf16[256,1024]{1,0:T(8,128)(2,1)S(1)} %get-tuple-element.7.refs_1_, bf16[256,1024]{1,0:T(8,128)(2,1)S(1)} %get-tuple-element.8.refs_2_), custom_call_target="tpu_custom_call" | custom-call | tf_op jit(solution)/shard_map/pallas_call | solution.py:450
